TPU v7x, 32 devices: a whole 2x2x4 slice. The times are simulated.
32 devices in a mesh: groups: 1, ep: 32 (over z, y, x, core).
Axes of the slice: x: 2, y: 2, z: 4, core: 2. Of those that a mesh axis runs over, the one named last changes fastest.
Arguments:
- tokens: bfloat16 [256, 7168], P(('groups', 'ep')), may hold values from -6 to 6
- expert_ids: int32 [256, 2], P(('groups', 'ep')), may hold values from 0 to 3, all different within a row; in each aligned block of 8 rows (0 to 7, 8 to 15, ...) at most 8 rows name the same one
- affinity: float32 [256, 2], P(('groups', 'ep')), may hold values from 0.05 to 1
- w_gate: bfloat16 [32, 7168, 256], P('ep'), may hold values from -0.0625 to 0.0625
- w_up: bfloat16 [32, 7168, 256], P('ep'), may hold values from -0.0625 to 0.0625
- w_down: bfloat16 [32, 256, 7168], P('ep'), may hold values from -0.125 to 0.125
Outputs:
- moe_out: bfloat16 [256, 7168], P(('groups', 'ep'))
Inputs may be any that keep to these rules, and one draw needn't show every extreme that they name: `expert_ids`: each token names 2 different experts. Among the 8 tokens of one device no expert is named more than 8 times, and in every draw some device names some expert exactly 8 times.
All inputs are finite; a program needn't handle non-finite values.
Results may differ from a plain program's by a relative error of at most 0.008.
Values may be sent and summed in bfloat16 or wider, within the bound.
No kernel may reach another device: no remote copies, remote signals or barrier semaphores. Data moves between devices by JAX's collectives and lax.ppermute only.
A program may use at most 128 MiB of HBM per device.

v0:
```python
import jax
import jax.numpy as jnp
from jax import lax
from jax.sharding import PartitionSpec as P

SPLIT = 8


route_scale = 2.5


def slots_of(expert_ids, experts):
    flat = expert_ids.reshape(-1)
    onehot = (flat[:, None] == jnp.arange(experts, dtype=jnp.int32)[None, :]).astype(jnp.int32)
    earlier = jnp.cumsum(onehot, axis=0) - onehot
    return jnp.sum(earlier * onehot, axis=1).reshape(expert_ids.shape)


def body(tokens, expert_ids, affinity, w_gate, w_up, w_down):
    devices = lax.axis_size("ep")
    experts = devices // SPLIT
    tok_rows = tokens.shape[0]
    routes = expert_ids.shape[1]
    width = tokens.shape[1]
    capacity = min(tok_rows, max(2, 2 * tok_rows * routes // experts))
    route_weight = route_scale * affinity / jnp.sum(affinity, axis=1, keepdims=True)
    slot = slots_of(expert_ids, experts)
    slot_key = expert_ids * capacity + slot
    columns = jnp.arange(experts * capacity, dtype=jnp.int32)
    matches = slot_key[:, :, None] == columns[None, None, :]
    select = jnp.sum(matches.astype(jnp.float32), axis=1).astype(jnp.bfloat16)
    outgoing = jnp.repeat(
        jnp.dot(select.T, tokens, preferred_element_type=jnp.float32)
        .astype(jnp.bfloat16)
        .reshape(experts, capacity, width),
        SPLIT,
        axis=0,
    )
    received = lax.all_to_all(outgoing, "ep", split_axis=0, concat_axis=0, tiled=True)
    rows = received.reshape(-1, width)
    gate = jnp.dot(rows, w_gate[0], preferred_element_type=jnp.float32)
    up = jnp.dot(rows, w_up[0], preferred_element_type=jnp.float32)
    hidden = (jax.nn.silu(gate) * up).astype(jnp.bfloat16)
    partial_value = jnp.dot(hidden, w_down[0], preferred_element_type=jnp.float32).astype(
        jnp.bfloat16
    )
    back = lax.all_to_all(
        partial_value.reshape(received.shape), "ep", split_axis=0, concat_axis=0, tiled=True
    )
    summed = jnp.sum(back.reshape(experts, SPLIT, capacity, width), axis=1, dtype=jnp.float32)
    combine = jnp.sum(jnp.where(matches, route_weight[:, :, None], 0.0), axis=1)
    mixed = jnp.dot(
        combine,
        summed.reshape(experts * capacity, width),
        precision=lax.Precision.HIGHEST,
        preferred_element_type=jnp.float32,
    )
    return mixed.astype(jnp.bfloat16)


def solution(mesh):
    return jax.shard_map(
        body,
        mesh=mesh,
        in_specs=(
            P(("groups", "ep"), None),
            P(("groups", "ep"), None),
            P(("groups", "ep"), None),
            P("ep", None, None),
            P("ep", None, None),
            P("ep", None, None),
        ),
        out_specs=P(("groups", "ep"), None),
        check_vma=False,
    )
```

profile of v0, /device:TPU:0, one launch (start us, length us, event | category | flops | bytes accessed | tf_op | source)
XLA Modules:
  0.0 194.5 jit_solution(15565348278835198464)
XLA Ops:
  0.0 0.0 copy-start
  0.0 0.7 reduce_sum.46
  0.7 0.7 multiply_divide_fusion
  1.4 0.8 copy.13
  2.2 0.1 eq.28
  2.3 0.1 fusion.30
  2.4 0.2 select_reduce_fusion.1
  2.6 0.1 reshape.25
  2.6 0.1 copy.15
  2.7 0.1 convert_reduce_fusion.1
  2.8 0.0 copy-done
  2.8 0.3 fusion.1
  3.1 0.4 broadcast_in_dim.22
  3.6 0.0 copy-start.2
  3.6 90.2 %all_to_all.10 = bf16[32,8,7168]{2,1,0:T(8,128)(2,1)S(1)} all-to-all(bf16[32,8,7168]{2,1,0:T(8,128)(2,1)S(1)} %bitcast.40), channel_id=1, replica_groups=mesh['groups'=1,'ep'=32] {'ep'}, dimensions={0} | all-to-all | bytes 7340032 | tf_op jit(solution)/shard_map/all_to_all | solution.py:39
  93.7 0.0 copy-start.1
  93.7 1.8 copy-done.1
  95.5 0.0 copy-done.2
  95.5 1.1 fusion.5
  96.6 10.0 %fusion = bf16[32,8,7168]{2,1,0:T(8,128)(2,1)} fusion(bf16[1,256,7168]{2,1,0:T(8,128)(2,1)} %param.11, bf16[1,7168,256]{2,1,0:T(8,128)(2,1)} %param.10, bf16[32,8,7168]{2,1,0:T(8,128)(2,1)} %copy-done.1, f32[256,256]{1,0:T(8,128)S(1)} %fusion.5), kind=kOutput, calls=%fused_computation.1 | convolution fusion | flops 1881276416 | bytes 14942208 | tf_op jit(solution)/shard_map/dot_general | solution.py:44
  106.7 86.1 %all_to_all.11 = bf16[32,8,7168]{2,1,0:T(8,128)(2,1)S(1)} all-to-all(bf16[32,8,7168]{2,1,0:T(8,128)(2,1)} %fusion), channel_id=1, replica_groups=mesh['groups'=1,'ep'=32] {'ep'}, dimensions={0} | all-to-all | bytes 7340032 | tf_op jit(solution)/shard_map/all_to_all | solution.py:47
  192.7 0.6 convert_reduce_fusion
  193.3 1.2 convolution_convert_fusion.2
  (2 shorter events, 0.0 us)
Async XLA Ops:
  0.0 2.8 %copy-start = (bf16[8,7168]{1,0:T(8,128)(2,1)S(1)}, bf16[8,7168]{1,0:T(8,128)(2,1)}, u32[]{:S(2)}) copy-start(bf16[8,7168]{1,0:T(8,128)(2,1)} %param.6) | copy-start | bytes 344068
  3.6 92.0 %copy-start.2 = (bf16[1,7168,256]{2,1,0:T(8,128)(2,1)S(1)}, bf16[1,7168,256]{2,1,0:T(8,128)(2,1)}, u32[]{:S(2)}) copy-start(bf16[1,7168,256]{2,1,0:T(8,128)(2,1)} %param.9) | copy-start | bytes 11010052
  93.7 1.8 copy-start.1
where the time goes:
time: 195 us; the launch traced here: 194 us
  blocking collectives  176 us (90%)
  matrix products  12.7 us (7%)
  local copies, waits for them, and re-layouts  3.21 us (2%)
  other arithmetic  2.36 us (1%)
    all_to_all x1, blocking collectives, body(): lax.all_to_all(outgoing, 'ep', split_axis=0, concat_axis=0, tiled=True)  90.2 us
    all_to_all x1, blocking collectives, body(): lax.all_to_all(partial_value.reshape(received.shape), 'ep', split_axis=0,...  86.1 us
    dot_general x1, matrix products, body(): jnp.dot(hidden, w_down[0], preferred_element_type=jnp.float32)  10 us

commit v1 on v0

v1 whole, which is shorter than its diff:
```python
import jax
import jax.numpy as jnp
from jax import lax
from jax.sharding import PartitionSpec as P

SPLIT = 8
CHUNKS = 2


route_scale = 2.5


def slots_of(expert_ids, experts):
    flat = expert_ids.reshape(-1)
    onehot = (flat[:, None] == jnp.arange(experts, dtype=jnp.int32)[None, :]).astype(jnp.int32)
    earlier = jnp.cumsum(onehot, axis=0) - onehot
    return jnp.sum(earlier * onehot, axis=1).reshape(expert_ids.shape)


def body(tokens, expert_ids, affinity, w_gate, w_up, w_down):
    devices = lax.axis_size("ep")
    experts = devices // SPLIT
    tok_rows, width = tokens.shape
    routes = expert_ids.shape[1]
    capacity = min(tok_rows, max(2, 2 * tok_rows * routes // experts))
    packed = capacity < tok_rows

    def rotate(value, planes):
        pairs = [(i, (i + planes * SPLIT) % devices) for i in range(devices)]
        return lax.ppermute(value, "ep", pairs)

    def swap(value, bit):
        return lax.ppermute(value, "ep", [(i, i ^ bit) for i in range(devices)])

    cat = lambda parts: parts[0] if len(parts) == 1 else jnp.concatenate(parts, axis=0)

    route_weight = route_scale * affinity / jnp.sum(affinity, axis=1, keepdims=True)
    own_expert = lax.axis_index("ep") // SPLIT
    if packed:
        slot = slots_of(expert_ids, experts)

    def choose(k):
        expert = (own_expert + k) % experts
        named = expert_ids == expert
        if not packed:
            return None, jnp.sum(jnp.where(named, route_weight, 0.0), axis=1, keepdims=True)
        hit = (slot[:, :, None] == jnp.arange(capacity, dtype=jnp.int32)) & named[:, :, None]
        return (
            jnp.sum(hit.astype(jnp.float32), axis=1),
            jnp.sum(jnp.where(hit, route_weight[:, :, None], 0.0), axis=1),
        )

    selects = [choose(k) for k in range(experts)]

    def rows_for(k):
        if not packed:
            return tokens
        select = selects[k][0].astype(jnp.bfloat16)
        return jnp.dot(select.T, tokens, preferred_element_type=jnp.float32).astype(jnp.bfloat16)

    groups = [rows_for(0)] + [rotate(rows_for(k), k) for k in range(1, experts)]
    per_chunk = experts // CHUNKS

    def spread(first, second, bits):
        near = swap(first, bits[0])
        far = swap(cat([first, near]), bits[1])
        return cat([first, near, far])

    def collect(blocks, bits):
        half = blocks.shape[0] // 2
        kept = add(blocks[:half], swap(blocks[half:], bits[1]))
        half //= 2
        return add(kept[:half], swap(kept[half:], bits[0]))

    def add(a, b):
        return (a.astype(jnp.float32) + b.astype(jnp.float32)).astype(jnp.bfloat16)

    def expert(rows):
        gate = jnp.dot(rows, w_gate[0], preferred_element_type=jnp.float32)
        up = jnp.dot(rows, w_up[0], preferred_element_type=jnp.float32)
        hidden = (jax.nn.silu(gate) * up).astype(jnp.bfloat16)
        return jnp.dot(hidden, w_down[0], preferred_element_type=jnp.float32)

    backs = []
    for chunk in range(CHUNKS):
        mine = range(chunk * per_chunk, (chunk + 1) * per_chunk)
        colours = [(list(mine[0::2]), (2, 4)), (list(mine[1::2]), (4, 2))]
        colours = [(members, bits) for members, bits in colours if members]
        here = cat([spread(cat([groups[g] for g in members]), None, bits) for members, bits in colours])
        size = here.shape[0]
        rows = cat([here, swap(here, 1)])
        partial_value = expert(rows).astype(jnp.bfloat16)
        chip = add(partial_value[:size], swap(partial_value[size:], 1))
        at = 0
        for members, bits in colours:
            count = 4 * len(members) * capacity
            got = collect(chip[at : at + count], bits)
            at += count
            for i, g in enumerate(members):
                backs.append((g, got[i * capacity : (i + 1) * capacity]))

    mixed = jnp.zeros((tok_rows, width), jnp.float32)
    for g, value in backs:
        home = (value if g == 0 else rotate(value, -g)).astype(jnp.float32)
        if packed:
            mixed = mixed + jnp.dot(
                selects[g][1], home, precision=lax.Precision.HIGHEST, preferred_element_type=jnp.float32
            )
        else:
            mixed = mixed + selects[g][1] * home
    return mixed.astype(jnp.bfloat16)


def solution(mesh):
    return jax.shard_map(
        body,
        mesh=mesh,
        in_specs=(
            P(("groups", "ep"), None),
            P(("groups", "ep"), None),
            P(("groups", "ep"), None),
            P("ep", None, None),
            P("ep", None, None),
            P("ep", None, None),
        ),
        out_specs=P(("groups", "ep"), None),
        check_vma=False,
    )
```

time: 195 us -> 83 us (0.43)
  blocking collectives: 176 us -> 0 us
  starting transfers between devices: 0 us -> 32.5 us
  waiting for transfers between devices: 0 us -> 23.6 us
  local copies, waits for them, and re-layouts: 3.21 us -> 7.58 us
  matrix products: 12.7 us -> 15 us
    all_to_all x2 -> x0, blocking collectives: 176 us -> none  [the longest x1 90.2 us: body(): lax.all_to_all(outgoing, 'ep', split_axis=0, concat_axis=0, tiled=True)]
    ppermute x0 -> x26, starting transfers between devices: none -> 32.5 us  [the longest x20 20.9 us: swap(): return lax.ppermute(value, 'ep', [(i, i ^ bit) for i in range(devices)])]
    ppermute x0 -> x26, waiting for transfers between devices: none -> 23.6 us  [the longest x20 18.9 us: swap(): return lax.ppermute(value, 'ep', [(i, i ^ bit) for i in range(devices)])]
    slice x0 -> x8, local copies, waits for them, and re-layouts: none -> 3.81 us  [the longest x2 3.71 us: body(): chip = add(partial_value[:size], swap(partial_value[size:], 1))]
    convert_element_type x1 -> x8, other arithmetic: 0.07 us -> 2.87 us  [the longest x7 2.08 us: add(): return (a.astype(jnp.float32) + b.astype(jnp.float32)).astype(jnp.bfloat16)]
    dot_general x4, matrix products: 12.7 us -> 15 us  [the longest x2 13.6 us: expert(): return jnp.dot(hidden, w_down[0], preferred_element_type=jnp.float32)]
  transfers between devices with their start and end apart: 0 -> 26, of which waited for: 0 -> 13; matrix products, arithmetic and copies ran while one was open for 0% -> 28% of each run, Pallas kernels for 0% -> 0%
where the time goes in v1:
time: 83 us; the launch traced here: 82.8 us
  starting transfers between devices  32.5 us (39%)
  waiting for transfers between devices  23.6 us (28%)
  matrix products  15 us (18%)
  local copies, waits for them, and re-layouts  7.58 us (9%)
  other arithmetic  3.88 us (5%)
    ppermute x20, starting transfers between devices, swap(): return lax.ppermute(value, 'ep', [(i, i ^ bit) for i in range(devices)])  20.9 us
    ppermute x20, waiting for transfers between devices, swap(): return lax.ppermute(value, 'ep', [(i, i ^ bit) for i in range(devices)])  18.9 us
    dot_general x2, matrix products, expert(): return jnp.dot(hidden, w_down[0], preferred_element_type=jnp.float32)  13.6 us
    ppermute x6, starting transfers between devices, rotate(): return lax.ppermute(value, 'ep', pairs)  11.6 us
    ppermute x6, waiting for transfers between devices, rotate(): return lax.ppermute(value, 'ep', pairs)  4.68 us
    slice x2, local copies, waits for them, and re-layouts, body(): chip = add(partial_value[:size], swap(partial_value[size:], 1))  3.71 us
    unnamed x26, local copies, waits for them, and re-layouts  3.59 us
    convert_element_type x7, other arithmetic, add(): return (a.astype(jnp.float32) + b.astype(jnp.float32)).astype(jnp.bfloat16)  2.08 us
  transfers between devices with their start and end apart: 26, of which 13 were waited for; matrix products, arithmetic and copies ran while one was open for 28% of the time, Pallas kernels for 0%

profile of v1, /device:TPU:0, one launch (start us, length us, event | category | flops | bytes accessed | tf_op | source)
XLA Modules:
  0.0 82.8 jit_solution(11213750121709656716)
XLA Ops:
  0.0 4.1 %collective-permute-start.12 = (bf16[8,7168]{1,0:T(8,128)(2,1)}, bf16[8,7168]{1,0:T(8,128)(2,1)S(1)}, u32[]{:S(2)}, u32[]{:S(2)}) collective-permute-start(bf16[8,7168]{1,0:T(8,128)(2,1)} %param.6), channel_id=1, source_target_pairs={{0,16},{1,17},{2,18},{3,19},{4,20},{5,21},{6,22},{7,23},{8,24},{9,... | collective-permute-start | bytes 344072 | tf_op jit(solution)/shard_map/ppermute | solution.py:30
  4.1 1.3 %collective-permute-start.15 = (bf16[8,7168]{1,0:T(8,128)(2,1)}, bf16[8,7168]{1,0:T(8,128)(2,1)S(1)}, u32[]{:S(2)}, u32[]{:S(2)}) collective-permute-start(bf16[8,7168]{1,0:T(8,128)(2,1)} %param.6), channel_id=1, source_target_pairs={{0,24},{1,25},{2,26},{3,27},{4,28},{5,29},{6,30},{7,31},{8,0},{9,1... | collective-permute-start | bytes 344072 | tf_op jit(solution)/shard_map/ppermute | solution.py:30
  5.4 1.5 %collective-permute-start = (bf16[8,7168]{1,0:T(8,128)(2,1)}, bf16[8,7168]{1,0:T(8,128)(2,1)S(1)}, u32[]{:S(2)}, u32[]{:S(2)}) collective-permute-start(bf16[8,7168]{1,0:T(8,128)(2,1)} %param.6), channel_id=1, source_target_pairs={{0,2},{1,3},{2,0},{3,1},{4,6},{5,7},{6,4},{7,5},{8,10},{9,11},{10,... | collective-permute-start | bytes 344072 | tf_op jit(solution)/shard_map/ppermute | solution.py:33
  8.6 1.8 %collective-permute-done = bf16[8,7168]{1,0:T(8,128)(2,1)S(1)} collective-permute-done((bf16[8,7168]{1,0:T(8,128)(2,1)}, bf16[8,7168]{1,0:T(8,128)(2,1)S(1)}, u32[]{:S(2)}, u32[]{:S(2)}) %collective-permute-start) | collective-permute-done | bytes 114720 | tf_op jit(solution)/shard_map/ppermute | solution.py:33
  11.3 1.6 %collective-permute-start.1 = (bf16[16,7168]{1,0:T(8,128)(2,1)S(1)}, bf16[16,7168]{1,0:T(8,128)(2,1)S(1)}, u32[]{:S(2)}, u32[]{:S(2)}) collective-permute-start(bf16[16,7168]{1,0:T(8,128)(2,1)S(1)} %pad_maximum_fusion), channel_id=1, source_target_pairs={{0,4},{1,5},{2,6},{3,7},{4,0},{5,1},{6,2},{7,3},{8,12},{9,13},{10,... | collective-permute-start | bytes 688136 | tf_op jit(solution)/shard_map/ppermute | solution.py:33
  12.9 2.1 %collective-permute-start.13 = (bf16[8,7168]{1,0:T(8,128)(2,1)S(1)}, bf16[8,7168]{1,0:T(8,128)(2,1)S(1)}, u32[]{:S(2)}, u32[]{:S(2)}) collective-permute-start(bf16[8,7168]{1,0:T(8,128)(2,1)S(1)} %collective-permute-done.12), channel_id=1, source_target_pairs={{0,2},{1,3},{2,0},{3,1},{4,6},{5,7},{6,4},{7,5},{8,10},{9,11},{10,... | collective-permute-start | bytes 344072 | tf_op jit(solution)/shard_map/ppermute | solution.py:33
  15.1 1.5 %collective-permute-start.16 = (bf16[8,7168]{1,0:T(8,128)(2,1)S(1)}, bf16[8,7168]{1,0:T(8,128)(2,1)S(1)}, u32[]{:S(2)}, u32[]{:S(2)}) collective-permute-start(bf16[8,7168]{1,0:T(8,128)(2,1)S(1)} %collective-permute-done.15), channel_id=1, source_target_pairs={{0,4},{1,5},{2,6},{3,7},{4,0},{5,1},{6,2},{7,3},{8,12},{9,13},{10,... | collective-permute-start | bytes 344072 | tf_op jit(solution)/shard_map/ppermute | solution.py:33
  17.9 1.6 %collective-permute-start.14 = (bf16[16,7168]{1,0:T(8,128)(2,1)S(1)}, bf16[16,7168]{1,0:T(8,128)(2,1)S(1)}, u32[]{:S(2)}, u32[]{:S(2)}) collective-permute-start(bf16[16,7168]{1,0:T(8,128)(2,1)S(1)} %pad_maximum_fusion.2), channel_id=1, source_target_pairs={{0,4},{1,5},{2,6},{3,7},{4,0},{5,1},{6,2},{7,3},{8,12},{9,13},{10,... | collective-permute-start | bytes 688136 | tf_op jit(solution)/shard_map/ppermute | solution.py:33
  19.4 2.9 %collective-permute-done.16 = bf16[8,7168]{1,0:T(8,128)(2,1)S(1)} collective-permute-done((bf16[8,7168]{1,0:T(8,128)(2,1)S(1)}, bf16[8,7168]{1,0:T(8,128)(2,1)S(1)}, u32[]{:S(2)}, u32[]{:S(2)}) %collective-permute-start.16) | collective-permute-done | bytes 114720 | tf_op jit(solution)/shard_map/ppermute | solution.py:33
  22.4 1.6 %collective-permute-start.17 = (bf16[16,7168]{1,0:T(8,128)(2,1)S(1)}, bf16[16,7168]{1,0:T(8,128)(2,1)S(1)}, u32[]{:S(2)}, u32[]{:S(2)}) collective-permute-start(bf16[16,7168]{1,0:T(8,128)(2,1)S(1)} %pad_maximum_fusion.3), channel_id=1, source_target_pairs={{0,2},{1,3},{2,0},{3,1},{4,6},{5,7},{6,4},{7,5},{8,10},{9,11},{10,... | collective-permute-start | bytes 688136 | tf_op jit(solution)/shard_map/ppermute | solution.py:33
  24.8 1.5 %collective-permute-start.4 = (bf16[16,7168]{1,0:T(8,128)(2,1)S(1)}, bf16[16,7168]{1,0:T(8,128)(2,1)S(1)}, u32[]{:S(2)}, u32[]{:S(2)}) collective-permute-start(bf16[16,7168]{1,0:T(8,128)(2,1)S(1)} %pad_maximum_fusion.1), channel_id=1, source_target_pairs={{0,2},{1,3},{2,0},{3,1},{4,6},{5,7},{6,4},{7,5},{8,10},{9,11},{10,... | collective-permute-start | bytes 688136 | tf_op jit(solution)/shard_map/ppermute | solution.py:33
  27.3 1.1 %collective-permute-done.17 = bf16[16,7168]{1,0:T(8,128)(2,1)S(1)} collective-permute-done((bf16[16,7168]{1,0:T(8,128)(2,1)S(1)}, bf16[16,7168]{1,0:T(8,128)(2,1)S(1)}, u32[]{:S(2)}, u32[]{:S(2)}) %collective-permute-start.17) | collective-permute-done | bytes 229408 | tf_op jit(solution)/shard_map/ppermute | solution.py:33
  28.6 2.3 %collective-permute-done.4 = bf16[16,7168]{1,0:T(8,128)(2,1)S(1)} collective-permute-done((bf16[16,7168]{1,0:T(8,128)(2,1)S(1)}, bf16[16,7168]{1,0:T(8,128)(2,1)S(1)}, u32[]{:S(2)}, u32[]{:S(2)}) %collective-permute-start.4) | collective-permute-done | bytes 229408 | tf_op jit(solution)/shard_map/ppermute | solution.py:33
  31.9 1.2 %copy-done.2 = bf16[128,7168]{1,0:T(8,128)(2,1)} copy-done((bf16[128,7168]{1,0:T(8,128)(2,1)}, bf16[128,7168]{1,0:T(8,128)(2,1)S(1)}, u32[]{:S(2)}) %copy-start.2) | copy-done | bytes 1835032
  33.8 7.1 %convolution_convert_fusion = bf16[128,7168]{1,0:T(8,128)(2,1)} fusion(bf16[1,256,7168]{2,1,0:T(8,128)(2,1)} %param.11, f32[128,256]{1,0:T(8,128)S(1)} %fusion.2, bf16[128,7168]{1,0:T(8,128)(2,1)} %copy-done.2, bf16[1,7168,256]{2,1,0:T(8,128)(2,1)} %param.9), kind=kOutput, calls=%fused_computation | convolution fusion | flops 940638208 | bytes 11141120 | tf_op jit(solution)/shard_map/dot_general | solution.py:82
  40.9 2.3 %slice.103 = bf16[64,7168]{1,0:T(8,128)(2,1)} slice(bf16[128,7168]{1,0:T(8,128)(2,1)} %convolution_convert_fusion), slice={[64:128], [0:7168]} | slice | bytes 1835008 | tf_op jit(solution)/shard_map/slice | solution.py:93
  44.5 6.5 %convolution_convert_fusion.1 = bf16[128,7168]{1,0:T(8,128)(2,1)} fusion(bf16[1,256,7168]{2,1,0:T(8,128)(2,1)} %param.11, f32[128,256]{1,0:T(8,128)S(1)} %fusion.4, bf16[128,7168]{1,0:T(8,128)(2,1)S(1)} %constant_dynamic-update-slice_fusion.6, bf16[1,7168,256]{2,1,0:T(8,128)(2,1)} %param.9), kind=kOutput, calls=%fused_computation.1 | convolution fusion | flops 940638208 | bytes 11141120 | tf_op jit(solution)/shard_map/dot_general | solution.py:82
  51.1 1.4 %slice.93 = bf16[64,7168]{1,0:T(8,128)(2,1)S(1)} slice(bf16[128,7168]{1,0:T(8,128)(2,1)} %convolution_convert_fusion.1), slice={[64:128], [0:7168]} | slice | bytes 1835008 | tf_op jit(solution)/shard_map/slice | solution.py:93
  52.8 1.6 %add_convert_fusion = bf16[64,7168]{1,0:T(8,128)(2,1)S(1)} fusion(bf16[64,7168]{1,0:T(8,128)(2,1)} %collective-permute-done.19, bf16[128,7168]{1,0:T(8,128)(2,1)S(1)} %copy-done.4), kind=kLoop, calls=%fused_computation.12 | loop fusion | flops 1835008 | bytes 2752512 | tf_op jit(solution)/shard_map/convert_element_type | solution.py:76
  54.4 1.6 %collective-permute-start.20 = (bf16[16,7168]{1,0:T(8,128)(2,1)S(1)}, bf16[16,7168]{1,0:T(8,128)(2,1)S(1)}, u32[]{:S(2)}, u32[]{:S(2)}) collective-permute-start(bf16[16,7168]{1,0:T(8,128)(2,1)S(1)} %get-tuple-element.15), channel_id=1, source_target_pairs={{0,4},{1,5},{2,6},{3,7},{4,0},{5,1},{6,2},{7,3},{8,12},{9,13},{10,... | collective-permute-start | bytes 688136 | tf_op jit(solution)/shard_map/ppermute | solution.py:33
  56.0 1.5 %collective-permute-start.23 = (bf16[16,7168]{1,0:T(8,128)(2,1)S(1)}, bf16[16,7168]{1,0:T(8,128)(2,1)S(1)}, u32[]{:S(2)}, u32[]{:S(2)}) collective-permute-start(bf16[16,7168]{1,0:T(8,128)(2,1)S(1)} %get-tuple-element.16), channel_id=1, source_target_pairs={{0,2},{1,3},{2,0},{3,1},{4,6},{5,7},{6,4},{7,5},{8,10},{9,11},{10,... | collective-permute-start | bytes 688136 | tf_op jit(solution)/shard_map/ppermute | solution.py:33
  58.9 4.1 %collective-permute-done.20 = bf16[16,7168]{1,0:T(8,128)(2,1)S(1)} collective-permute-done((bf16[16,7168]{1,0:T(8,128)(2,1)S(1)}, bf16[16,7168]{1,0:T(8,128)(2,1)S(1)}, u32[]{:S(2)}, u32[]{:S(2)}) %collective-permute-start.20) | collective-permute-done | bytes 229408 | tf_op jit(solution)/shard_map/ppermute | solution.py:33
  63.0 1.5 %collective-permute-done.23 = bf16[16,7168]{1,0:T(8,128)(2,1)S(1)} collective-permute-done((bf16[16,7168]{1,0:T(8,128)(2,1)S(1)}, bf16[16,7168]{1,0:T(8,128)(2,1)S(1)}, u32[]{:S(2)}, u32[]{:S(2)}) %collective-permute-start.23) | collective-permute-done | bytes 229408 | tf_op jit(solution)/shard_map/ppermute | solution.py:33
  65.2 1.6 %collective-permute-start.21 = (bf16[8,7168]{1,0:T(8,128)(2,1)S(1)}, bf16[8,7168]{1,0:T(8,128)(2,1)S(1)}, u32[]{:S(2)}, u32[]{:S(2)}) collective-permute-start(bf16[8,7168]{1,0:T(8,128)(2,1)S(1)} %slice.107), channel_id=1, source_target_pairs={{0,2},{1,3},{2,0},{3,1},{4,6},{5,7},{6,4},{7,5},{8,10},{9,11},{10,... | collective-permute-start | bytes 344072 | tf_op jit(solution)/shard_map/ppermute | solution.py:33
  66.8 1.1 %collective-permute-done.7 = bf16[16,7168]{1,0:T(8,128)(2,1)S(1)} collective-permute-done((bf16[16,7168]{1,0:T(8,128)(2,1)S(1)}, bf16[16,7168]{1,0:T(8,128)(2,1)S(1)}, u32[]{:S(2)}, u32[]{:S(2)}) %collective-permute-start.7) | collective-permute-done | bytes 229408 | tf_op jit(solution)/shard_map/ppermute | solution.py:33
  67.9 1.5 %collective-permute-done.9 = bf16[16,7168]{1,0:T(8,128)(2,1)S(1)} collective-permute-done((bf16[16,7168]{1,0:T(8,128)(2,1)S(1)}, bf16[16,7168]{1,0:T(8,128)(2,1)S(1)}, u32[]{:S(2)}, u32[]{:S(2)}) %collective-permute-start.9) | collective-permute-done | bytes 229408 | tf_op jit(solution)/shard_map/ppermute | solution.py:33
  70.1 1.6 %collective-permute-start.8 = (bf16[8,7168]{1,0:T(8,128)(2,1)S(1)}, bf16[8,7168]{1,0:T(8,128)(2,1)S(1)}, u32[]{:S(2)}, u32[]{:S(2)}) collective-permute-start(bf16[8,7168]{1,0:T(8,128)(2,1)S(1)} %slice.97), channel_id=1, source_target_pairs={{0,2},{1,3},{2,0},{3,1},{4,6},{5,7},{6,4},{7,5},{8,10},{9,11},{10,... | collective-permute-start | bytes 344072 | tf_op jit(solution)/shard_map/ppermute | solution.py:33
  71.7 1.2 %collective-permute-start.25 = (bf16[8,7168]{1,0:T(8,128)(2,1)S(1)}, bf16[8,7168]{1,0:T(8,128)(2,1)S(1)}, u32[]{:S(2)}, u32[]{:S(2)}) collective-permute-start(bf16[8,7168]{1,0:T(8,128)(2,1)S(1)} %add_convert_fusion.7), channel_id=1, source_target_pairs={{0,8},{1,9},{2,10},{3,11},{4,12},{5,13},{6,14},{7,15},{8,16},{9,17... | collective-permute-start | bytes 344072 | tf_op jit(solution)/shard_map/ppermute | solution.py:30
  73.0 2.5 %collective-permute-start.22 = (bf16[8,7168]{1,0:T(8,128)(2,1)S(1)}, bf16[8,7168]{1,0:T(8,128)(2,1)S(1)}, u32[]{:S(2)}, u32[]{:S(2)}) collective-permute-start(bf16[8,7168]{1,0:T(8,128)(2,1)S(1)} %add_convert_fusion.8), channel_id=1, source_target_pairs={{0,16},{1,17},{2,18},{3,19},{4,20},{5,21},{6,22},{7,23},{8,24},{9,... | collective-permute-start | bytes 344072 | tf_op jit(solution)/shard_map/ppermute | solution.py:30
  75.6 1.7 %collective-permute-start.11 = (bf16[8,7168]{1,0:T(8,128)(2,1)S(1)}, bf16[8,7168]{1,0:T(8,128)(2,1)S(1)}, u32[]{:S(2)}, u32[]{:S(2)}) collective-permute-start(bf16[8,7168]{1,0:T(8,128)(2,1)S(1)} %add_convert_fusion.9), channel_id=1, source_target_pairs={{0,24},{1,25},{2,26},{3,27},{4,28},{5,29},{6,30},{7,31},{8,0},{9,1... | collective-permute-start | bytes 344072 | tf_op jit(solution)/shard_map/ppermute | solution.py:30
  77.3 1.1 %collective-permute-done.25 = bf16[8,7168]{1,0:T(8,128)(2,1)S(1)} collective-permute-done((bf16[8,7168]{1,0:T(8,128)(2,1)S(1)}, bf16[8,7168]{1,0:T(8,128)(2,1)S(1)}, u32[]{:S(2)}, u32[]{:S(2)}) %collective-permute-start.25) | collective-permute-done | bytes 114720 | tf_op jit(solution)/shard_map/ppermute | solution.py:30
  78.5 3.5 %collective-permute-done.22 = bf16[8,7168]{1,0:T(8,128)(2,1)S(1)} collective-permute-done((bf16[8,7168]{1,0:T(8,128)(2,1)S(1)}, bf16[8,7168]{1,0:T(8,128)(2,1)S(1)}, u32[]{:S(2)}, u32[]{:S(2)}) %collective-permute-start.22) | collective-permute-done | bytes 114720 | tf_op jit(solution)/shard_map/ppermute | solution.py:30
  (76 shorter events, 12.9 us)
Async XLA Ops:
  0.0 12.9 %collective-permute-start.12 = (bf16[8,7168]{1,0:T(8,128)(2,1)}, bf16[8,7168]{1,0:T(8,128)(2,1)S(1)}, u32[]{:S(2)}, u32[]{:S(2)}) collective-permute-start(bf16[8,7168]{1,0:T(8,128)(2,1)} %param.6), channel_id=1, source_target_pairs={{0,16},{1,17},{2,18},{3,19},{4,20},{5,21},{6,22},{7,23},{8,24},{9,... | collective-permute-start | bytes 344072 | tf_op jit(solution)/shard_map/ppermute | solution.py:30
  4.1 11.0 %collective-permute-start.15 = (bf16[8,7168]{1,0:T(8,128)(2,1)}, bf16[8,7168]{1,0:T(8,128)(2,1)S(1)}, u32[]{:S(2)}, u32[]{:S(2)}) collective-permute-start(bf16[8,7168]{1,0:T(8,128)(2,1)} %param.6), channel_id=1, source_target_pairs={{0,24},{1,25},{2,26},{3,27},{4,28},{5,29},{6,30},{7,31},{8,0},{9,1... | collective-permute-start | bytes 344072 | tf_op jit(solution)/shard_map/ppermute | solution.py:30
  5.4 5.0 %collective-permute-start = (bf16[8,7168]{1,0:T(8,128)(2,1)}, bf16[8,7168]{1,0:T(8,128)(2,1)S(1)}, u32[]{:S(2)}, u32[]{:S(2)}) collective-permute-start(bf16[8,7168]{1,0:T(8,128)(2,1)} %param.6), channel_id=1, source_target_pairs={{0,2},{1,3},{2,0},{3,1},{4,6},{5,7},{6,4},{7,5},{8,10},{9,11},{10,... | collective-permute-start | bytes 344072 | tf_op jit(solution)/shard_map/ppermute | solution.py:33
  6.9 9.7 %collective-permute-start.2 = (bf16[8,7168]{1,0:T(8,128)(2,1)}, bf16[8,7168]{1,0:T(8,128)(2,1)S(1)}, u32[]{:S(2)}, u32[]{:S(2)}) collective-permute-start(bf16[8,7168]{1,0:T(8,128)(2,1)} %param.6), channel_id=1, source_target_pairs={{0,8},{1,9},{2,10},{3,11},{4,12},{5,13},{6,14},{7,15},{8,16},{9,17... | collective-permute-start | bytes 344072 | tf_op jit(solution)/shard_map/ppermute | solution.py:30
  11.3 15.0 %collective-permute-start.1 = (bf16[16,7168]{1,0:T(8,128)(2,1)S(1)}, bf16[16,7168]{1,0:T(8,128)(2,1)S(1)}, u32[]{:S(2)}, u32[]{:S(2)}) collective-permute-start(bf16[16,7168]{1,0:T(8,128)(2,1)S(1)} %pad_maximum_fusion), channel_id=1, source_target_pairs={{0,4},{1,5},{2,6},{3,7},{4,0},{5,1},{6,2},{7,3},{8,12},{9,13},{10,... | collective-permute-start | bytes 688136 | tf_op jit(solution)/shard_map/ppermute | solution.py:33
  12.9 4.9 %collective-permute-start.13 = (bf16[8,7168]{1,0:T(8,128)(2,1)S(1)}, bf16[8,7168]{1,0:T(8,128)(2,1)S(1)}, u32[]{:S(2)}, u32[]{:S(2)}) collective-permute-start(bf16[8,7168]{1,0:T(8,128)(2,1)S(1)} %collective-permute-done.12), channel_id=1, source_target_pairs={{0,2},{1,3},{2,0},{3,1},{4,6},{5,7},{6,4},{7,5},{8,10},{9,11},{10,... | collective-permute-start | bytes 344072 | tf_op jit(solution)/shard_map/ppermute | solution.py:33
  15.1 7.3 %collective-permute-start.16 = (bf16[8,7168]{1,0:T(8,128)(2,1)S(1)}, bf16[8,7168]{1,0:T(8,128)(2,1)S(1)}, u32[]{:S(2)}, u32[]{:S(2)}) collective-permute-start(bf16[8,7168]{1,0:T(8,128)(2,1)S(1)} %collective-permute-done.15), channel_id=1, source_target_pairs={{0,4},{1,5},{2,6},{3,7},{4,0},{5,1},{6,2},{7,3},{8,12},{9,13},{10,... | collective-permute-start | bytes 344072 | tf_op jit(solution)/shard_map/ppermute | solution.py:33
  16.6 8.2 %collective-permute-start.3 = (bf16[8,7168]{1,0:T(8,128)(2,1)S(1)}, bf16[8,7168]{1,0:T(8,128)(2,1)S(1)}, u32[]{:S(2)}, u32[]{:S(2)}) collective-permute-start(bf16[8,7168]{1,0:T(8,128)(2,1)S(1)} %collective-permute-done.2), channel_id=1, source_target_pairs={{0,4},{1,5},{2,6},{3,7},{4,0},{5,1},{6,2},{7,3},{8,12},{9,13},{10,... | collective-permute-start | bytes 344072 | tf_op jit(solution)/shard_map/ppermute | solution.py:33
  17.9 9.4 %collective-permute-start.14 = (bf16[16,7168]{1,0:T(8,128)(2,1)S(1)}, bf16[16,7168]{1,0:T(8,128)(2,1)S(1)}, u32[]{:S(2)}, u32[]{:S(2)}) collective-permute-start(bf16[16,7168]{1,0:T(8,128)(2,1)S(1)} %pad_maximum_fusion.2), channel_id=1, source_target_pairs={{0,4},{1,5},{2,6},{3,7},{4,0},{5,1},{6,2},{7,3},{8,12},{9,13},{10,... | collective-permute-start | bytes 688136 | tf_op jit(solution)/shard_map/ppermute | solution.py:33
  22.4 6.1 %collective-permute-start.17 = (bf16[16,7168]{1,0:T(8,128)(2,1)S(1)}, bf16[16,7168]{1,0:T(8,128)(2,1)S(1)}, u32[]{:S(2)}, u32[]{:S(2)}) collective-permute-start(bf16[16,7168]{1,0:T(8,128)(2,1)S(1)} %pad_maximum_fusion.3), channel_id=1, source_target_pairs={{0,2},{1,3},{2,0},{3,1},{4,6},{5,7},{6,4},{7,5},{8,10},{9,11},{10,... | collective-permute-start | bytes 688136 | tf_op jit(solution)/shard_map/ppermute | solution.py:33
  24.8 6.1 %collective-permute-start.4 = (bf16[16,7168]{1,0:T(8,128)(2,1)S(1)}, bf16[16,7168]{1,0:T(8,128)(2,1)S(1)}, u32[]{:S(2)}, u32[]{:S(2)}) collective-permute-start(bf16[16,7168]{1,0:T(8,128)(2,1)S(1)} %pad_maximum_fusion.1), channel_id=1, source_target_pairs={{0,2},{1,3},{2,0},{3,1},{4,6},{5,7},{6,4},{7,5},{8,10},{9,11},{10,... | collective-permute-start | bytes 688136 | tf_op jit(solution)/shard_map/ppermute | solution.py:33
  27.3 5.9 %copy-start = (bf16[1,7168,256]{2,1,0:T(8,128)(2,1)S(1)}, bf16[1,7168,256]{2,1,0:T(8,128)(2,1)}, u32[]{:S(2)}) copy-start(bf16[1,7168,256]{2,1,0:T(8,128)(2,1)} %param.10) | copy-start | bytes 11010052
  28.5 3.4 %collective-permute-start.18 = (bf16[64,7168]{1,0:T(8,128)(2,1)S(1)}, bf16[64,7168]{1,0:T(8,128)(2,1)S(1)}, u32[]{:S(2)}, u32[]{:S(2)}) collective-permute-start(bf16[64,7168]{1,0:T(8,128)(2,1)S(1)} %get-tuple-element.21), channel_id=1, source_target_pairs={{0,1},{1,0},{2,3},{3,2},{4,5},{5,4},{6,7},{7,6},{8,9},{9,8},{10,11... | collective-permute-start | bytes 2752520 | tf_op jit(solution)/shard_map/ppermute | solution.py:33
  31.9 11.9 %collective-permute-start.5 = (bf16[64,7168]{1,0:T(8,128)(2,1)}, bf16[64,7168]{1,0:T(8,128)(2,1)S(1)}, u32[]{:S(2)}, u32[]{:S(2)}) collective-permute-start(bf16[64,7168]{1,0:T(8,128)(2,1)} %copy-done.5), channel_id=1, source_target_pairs={{0,1},{1,0},{2,3},{3,2},{4,5},{5,4},{6,7},{7,6},{8,9},{9,8},{10,11... | collective-permute-start | bytes 2752520 | tf_op jit(solution)/shard_map/ppermute | solution.py:33
  40.9 2.9 %copy-start.1 = (bf16[1,7168,256]{2,1,0:T(8,128)(2,1)S(1)}, bf16[1,7168,256]{2,1,0:T(8,128)(2,1)}, u32[]{:S(2)}) copy-start(bf16[1,7168,256]{2,1,0:T(8,128)(2,1)} %param.10) | copy-start | bytes 11010052
  43.3 9.3 %collective-permute-start.19 = (bf16[64,7168]{1,0:T(8,128)(2,1)}, bf16[64,7168]{1,0:T(8,128)(2,1)}, u32[]{:S(2)}, u32[]{:S(2)}) collective-permute-start(bf16[64,7168]{1,0:T(8,128)(2,1)} %slice.103), channel_id=1, source_target_pairs={{0,1},{1,0},{2,3},{3,2},{4,5},{5,4},{6,7},{7,6},{8,9},{9,8},{10,11... | collective-permute-start | bytes 2752520 | tf_op jit(solution)/shard_map/ppermute | solution.py:33
  51.1 1.8 %copy-start.4 = (bf16[128,7168]{1,0:T(8,128)(2,1)S(1)}, bf16[128,7168]{1,0:T(8,128)(2,1)}, u32[]{:S(2)}) copy-start(bf16[128,7168]{1,0:T(8,128)(2,1)} %convolution_convert_fusion) | copy-start | bytes 5505028
  52.4 5.1 %copy-start.3 = (bf16[128,7168]{1,0:T(8,128)(2,1)S(1)}, bf16[128,7168]{1,0:T(8,128)(2,1)}, u32[]{:S(2)}) copy-start(bf16[128,7168]{1,0:T(8,128)(2,1)} %convolution_convert_fusion.1) | copy-start | bytes 5505028
  52.4 5.1 %collective-permute-start.6 = (bf16[64,7168]{1,0:T(8,128)(2,1)S(1)}, bf16[64,7168]{1,0:T(8,128)(2,1)S(1)}, u32[]{:S(2)}, u32[]{:S(2)}) collective-permute-start(bf16[64,7168]{1,0:T(8,128)(2,1)S(1)} %slice.93), channel_id=1, source_target_pairs={{0,1},{1,0},{2,3},{3,2},{4,5},{5,4},{6,7},{7,6},{8,9},{9,8},{10,11... | collective-permute-start | bytes 2752520 | tf_op jit(solution)/shard_map/ppermute | solution.py:33
  54.4 8.5 %collective-permute-start.20 = (bf16[16,7168]{1,0:T(8,128)(2,1)S(1)}, bf16[16,7168]{1,0:T(8,128)(2,1)S(1)}, u32[]{:S(2)}, u32[]{:S(2)}) collective-permute-start(bf16[16,7168]{1,0:T(8,128)(2,1)S(1)} %get-tuple-element.15), channel_id=1, source_target_pairs={{0,4},{1,5},{2,6},{3,7},{4,0},{5,1},{6,2},{7,3},{8,12},{9,13},{10,... | collective-permute-start | bytes 688136 | tf_op jit(solution)/shard_map/ppermute | solution.py:33
  56.0 8.5 %collective-permute-start.23 = (bf16[16,7168]{1,0:T(8,128)(2,1)S(1)}, bf16[16,7168]{1,0:T(8,128)(2,1)S(1)}, u32[]{:S(2)}, u32[]{:S(2)}) collective-permute-start(bf16[16,7168]{1,0:T(8,128)(2,1)S(1)} %get-tuple-element.16), channel_id=1, source_target_pairs={{0,2},{1,3},{2,0},{3,1},{4,6},{5,7},{6,4},{7,5},{8,10},{9,11},{10,... | collective-permute-start | bytes 688136 | tf_op jit(solution)/shard_map/ppermute | solution.py:33
  57.8 10.1 %collective-permute-start.7 = (bf16[16,7168]{1,0:T(8,128)(2,1)S(1)}, bf16[16,7168]{1,0:T(8,128)(2,1)S(1)}, u32[]{:S(2)}, u32[]{:S(2)}) collective-permute-start(bf16[16,7168]{1,0:T(8,128)(2,1)S(1)} %get-tuple-element.11), channel_id=1, source_target_pairs={{0,4},{1,5},{2,6},{3,7},{4,0},{5,1},{6,2},{7,3},{8,12},{9,13},{10,... | collective-permute-start | bytes 688136 | tf_op jit(solution)/shard_map/ppermute | solution.py:33
  58.3 11.1 %collective-permute-start.9 = (bf16[16,7168]{1,0:T(8,128)(2,1)S(1)}, bf16[16,7168]{1,0:T(8,128)(2,1)S(1)}, u32[]{:S(2)}, u32[]{:S(2)}) collective-permute-start(bf16[16,7168]{1,0:T(8,128)(2,1)S(1)} %get-tuple-element.12), channel_id=1, source_target_pairs={{0,2},{1,3},{2,0},{3,1},{4,6},{5,7},{6,4},{7,5},{8,10},{9,11},{10,... | collective-permute-start | bytes 688136 | tf_op jit(solution)/shard_map/ppermute | solution.py:33
  64.6 12.7 %copy-start.6 = (f32[8,2]{0,1:T(2,128)S(1)}, f32[8,2]{0,1:T(2,128)}, u32[]{:S(2)}) copy-start(f32[8,2]{0,1:T(2,128)} %param.8) | copy-start | bytes 196
  64.6 12.7 %copy-start.7 = (s32[8,2]{0,1:T(2,128)S(1)}, s32[8,2]{0,1:T(2,128)}, u32[]{:S(2)}) copy-start(s32[8,2]{0,1:T(2,128)} %param.7) | copy-start | bytes 196
  64.7 7.0 %collective-permute-start.24 = (bf16[8,7168]{1,0:T(8,128)(2,1)S(1)}, bf16[8,7168]{1,0:T(8,128)(2,1)S(1)}, u32[]{:S(2)}, u32[]{:S(2)}) collective-permute-start(bf16[8,7168]{1,0:T(8,128)(2,1)S(1)} %slice.111), channel_id=1, source_target_pairs={{0,4},{1,5},{2,6},{3,7},{4,0},{5,1},{6,2},{7,3},{8,12},{9,13},{10,... | collective-permute-start | bytes 344072 | tf_op jit(solution)/shard_map/ppermute | solution.py:33
  65.2 7.7 %collective-permute-start.21 = (bf16[8,7168]{1,0:T(8,128)(2,1)S(1)}, bf16[8,7168]{1,0:T(8,128)(2,1)S(1)}, u32[]{:S(2)}, u32[]{:S(2)}) collective-permute-start(bf16[8,7168]{1,0:T(8,128)(2,1)S(1)} %slice.107), channel_id=1, source_target_pairs={{0,2},{1,3},{2,0},{3,1},{4,6},{5,7},{6,4},{7,5},{8,10},{9,11},{10,... | collective-permute-start | bytes 344072 | tf_op jit(solution)/shard_map/ppermute | solution.py:33
  69.5 6.0 %collective-permute-start.10 = (bf16[8,7168]{1,0:T(8,128)(2,1)S(1)}, bf16[8,7168]{1,0:T(8,128)(2,1)S(1)}, u32[]{:S(2)}, u32[]{:S(2)}) collective-permute-start(bf16[8,7168]{1,0:T(8,128)(2,1)S(1)} %slice.101), channel_id=1, source_target_pairs={{0,4},{1,5},{2,6},{3,7},{4,0},{5,1},{6,2},{7,3},{8,12},{9,13},{10,... | collective-permute-start | bytes 344072 | tf_op jit(solution)/shard_map/ppermute | solution.py:33
  70.1 7.2 %collective-permute-start.8 = (bf16[8,7168]{1,0:T(8,128)(2,1)S(1)}, bf16[8,7168]{1,0:T(8,128)(2,1)S(1)}, u32[]{:S(2)}, u32[]{:S(2)}) collective-permute-start(bf16[8,7168]{1,0:T(8,128)(2,1)S(1)} %slice.97), channel_id=1, source_target_pairs={{0,2},{1,3},{2,0},{3,1},{4,6},{5,7},{6,4},{7,5},{8,10},{9,11},{10,... | collective-permute-start | bytes 344072 | tf_op jit(solution)/shard_map/ppermute | solution.py:33
  71.7 6.7 %collective-permute-start.25 = (bf16[8,7168]{1,0:T(8,128)(2,1)S(1)}, bf16[8,7168]{1,0:T(8,128)(2,1)S(1)}, u32[]{:S(2)}, u32[]{:S(2)}) collective-permute-start(bf16[8,7168]{1,0:T(8,128)(2,1)S(1)} %add_convert_fusion.7), channel_id=1, source_target_pairs={{0,8},{1,9},{2,10},{3,11},{4,12},{5,13},{6,14},{7,15},{8,16},{9,17... | collective-permute-start | bytes 344072 | tf_op jit(solution)/shard_map/ppermute | solution.py:30
  73.0 9.0 %collective-permute-start.22 = (bf16[8,7168]{1,0:T(8,128)(2,1)S(1)}, bf16[8,7168]{1,0:T(8,128)(2,1)S(1)}, u32[]{:S(2)}, u32[]{:S(2)}) collective-permute-start(bf16[8,7168]{1,0:T(8,128)(2,1)S(1)} %add_convert_fusion.8), channel_id=1, source_target_pairs={{0,16},{1,17},{2,18},{3,19},{4,20},{5,21},{6,22},{7,23},{8,24},{9,... | collective-permute-start | bytes 344072 | tf_op jit(solution)/shard_map/ppermute | solution.py:30
  75.6 6.4 %collective-permute-start.11 = (bf16[8,7168]{1,0:T(8,128)(2,1)S(1)}, bf16[8,7168]{1,0:T(8,128)(2,1)S(1)}, u32[]{:S(2)}, u32[]{:S(2)}) collective-permute-start(bf16[8,7168]{1,0:T(8,128)(2,1)S(1)} %add_convert_fusion.9), channel_id=1, source_target_pairs={{0,24},{1,25},{2,26},{3,27},{4,28},{5,29},{6,30},{7,31},{8,0},{9,1... | collective-permute-start | bytes 344072 | tf_op jit(solution)/shard_map/ppermute | solution.py:30
  (2 other events, 2.2 us)
